TPU v7x, 16 devices: a whole 2x2x2 slice. The times are simulated.
16 devices in a mesh: dp: 1, ep: 16 (over x, y, z, core).
Axes of the slice: x: 2, y: 2, z: 2, core: 2. Of those that a mesh axis runs over, the one named last changes fastest.
Arguments:
- x: bfloat16 [1, 16, 256, 1536], P('dp', 'ep')
- expert: int32 [1, 16, 256, 2], P('dp', 'ep')
- slot: int32 [1, 16, 256, 2], P('dp', 'ep')
- gate: float32 [1, 16, 256, 2], P('dp', 'ep')
- w_gate: bfloat16 [32, 1536, 9216], P('ep')
- w_up: bfloat16 [32, 1536, 9216], P('ep')
- w_down: bfloat16 [32, 9216, 1536], P('ep')
Outputs:
- y: bfloat16 [1, 16, 256, 1536], P('dp', 'ep')
All inputs are finite; a program needn't handle non-finite values.
Results may differ from a plain program's by a relative error of at most 0.009.
Values are sent between devices in bfloat16 or wider.
A program may use at most 2 GiB of HBM per device.

v0:
```python
import jax
import jax.numpy as jnp
from jax import lax
from jax.sharding import NamedSharding, PartitionSpec as P


def einsum(form, a, b):
    return jnp.einsum(form, a.astype(jnp.float32), b.astype(jnp.float32))


def solution(mesh):
    def placed(v, *spec):
        return lax.with_sharding_constraint(v, NamedSharding(mesh, P(*spec)))

    def step(x, expert, slot, gate, w_gate, w_up, w_down):
        experts, (tokens, top) = w_gate.shape[0], expert.shape[2:]
        slots = 5 * tokens * top // (4 * experts)
        to_expert = jax.nn.one_hot(expert, experts, dtype=jnp.bfloat16)
        to_slot = jax.nn.one_hot(slot, slots, dtype=jnp.bfloat16)
        weighted = to_expert * gate[..., None].astype(jnp.bfloat16)
        dispatch = einsum("abtke,abtkc->abtec", to_expert, to_slot).astype(jnp.bfloat16)
        combine = einsum("abtke,abtkc->abtec", weighted, to_slot).astype(jnp.bfloat16)
        z = einsum("abtec,abtd->aebcd", dispatch, x).astype(jnp.bfloat16)
        z = placed(z, "dp", None, "ep", None, None)
        z = placed(z, "dp", "ep", None, None, None)
        h = jax.nn.silu(einsum("aebcd,edf->aebcf", z, w_gate))
        h = (h * einsum("aebcd,edf->aebcf", z, w_up)).astype(jnp.bfloat16)
        out = einsum("aebcf,efd->aebcd", h, w_down).astype(jnp.bfloat16)
        out = placed(out, "dp", "ep", None, None, None)
        out = placed(out, "dp", None, "ep", None, None)
        y = einsum("abtec,aebcd->abtd", combine, out)
        return y.astype(jnp.bfloat16)

    return step
```

profile of v0, /device:TPU:0, one launch (start us, length us, event | category | flops | bytes accessed | tf_op | source)
XLA Modules:
  0.0 195.7 jit_solution(6372608657527156290)
XLA Ops:
  0.0 0.0 copy-start
  0.0 0.9 copy.11
  0.9 0.0 copy-start.2
  0.9 0.8 copy.9
  1.7 0.0 copy-done.2
  1.8 0.0 copy-start.4
  1.8 0.6 copy-done.4
  2.4 2.8 %convolution_convert_fusion.1 = bf16[256,32,20]{1,2,0:T(8,128)(2,1)S(1)} fusion(s32[256,2]{1,0:T(8,128)S(1)} %copy.11, s32[256,2]{1,0:T(8,128)S(1)} %copy.9), kind=kOutput, calls=%fused_computation.26 | convolution fusion | flops 845824 | bytes 331776 | tf_op jit(solution)/abtke,abtkc->abtec/dot_general | solution.py:8
  5.2 0.0 copy-done
  5.2 0.9 fusion.32
  6.1 1.8 reshape.52
  7.9 2.9 %copy.13 = bf16[1,16,2,1,20,1536]{5,2,4,3,0,1:T(2,128)(2,1)S(1)} copy(bf16[1,16,2,1,20,1536]{5,2,1,4,3,0:T(2,128)(2,1)} %reshape.52) | data formatting | bytes 3932160 | tf_op jit(solution)/sharding_constraint;jit(solution)/sharding_constraint | solution.py:13
  10.8 31.1 %all-to-all.4 = bf16[1,16,2,1,20,1536]{5,2,4,3,0,1:T(2,128)(2,1)S(1)} all-to-all(bf16[1,16,2,1,20,1536]{5,2,4,3,0,1:T(2,128)(2,1)S(1)} %copy.13), channel_id=1, replica_groups=mesh['dp'=1,'ep'=16] {'ep'}, dimensions={1} | all-to-all | bytes 3932160 | tf_op jit(solution)/sharding_constraint;jit(solution)/sharding_constraint | solution.py:13
  41.8 34.9 %fusion.4 = f32[2,16,20,9216]{3,2,1,0:T(8,128)} fusion(bf16[2,1536,9216]{2,1,0:T(8,128)(2,1)} %param.4, bf16[1,16,2,1,20,1536]{5,2,4,3,0,1:T(2,128)(2,1)S(1)} %all-to-all.4), kind=kOutput, calls=%fused_computation.4 | convolution fusion | flops 18119393280 | bytes 82182144 | tf_op jit(solution)/aebcd,edf->aebcf/dot_general | solution.py:8
  76.7 44.4 %fusion.68 = bf16[2,16,20,9216]{3,2,1,0:T(8,128)(2,1)} fusion(bf16[2,1536,9216]{2,1,0:T(8,128)(2,1)} %param.5, f32[2,16,20,9216]{3,2,1,0:T(8,128)} %fusion.4, bf16[1,16,2,1,20,1536]{5,2,4,3,0,1:T(2,128)(2,1)S(1)} %all-to-all.4), kind=kOutput, calls=%fused_computation.13.clone.clone.clone.clone.clone.1 | convolution fusion | flops 18154782720 | bytes 93978624 | tf_op jit(solution)/aebcd,edf->aebcf/dot_general | solution.py:8
  121.1 30.8 %fusion.25 = bf16[1,2,16,1,20,1536]{5,4,2,1,3,0:T(8,128)(2,1)S(1)} fusion(bf16[2,9216,1536]{2,1,0:T(8,128)(2,1)} %param.6, bf16[2,16,20,9216]{3,2,1,0:T(8,128)(2,1)} %fusion.68), kind=kOutput, calls=%fused_computation.17 | convolution fusion | flops 18120376320 | bytes 70385664 | tf_op jit(solution)/aebcf,efd->aebcd/dot_general | solution.py:8
  152.0 3.3 %copy.15 = bf16[1,2,16,1,20,1536]{5,1,4,3,0,2:T(2,128)(2,1)} copy(bf16[1,2,16,1,20,1536]{5,4,2,1,3,0:T(8,128)(2,1)S(1)} %fusion.25) | data formatting | bytes 3932160 | tf_op jit(solution)/sharding_constraint;jit(solution)/sharding_constraint | solution.py:13
  155.3 0.0 copy-start.6
  155.3 0.0 copy-start.3
  155.3 0.0 copy-start.5
  155.3 2.6 %all-to-all-start.1 = ((bf16[1,2,16,1,20,1536]{5,1,4,3,0,2:T(2,128)(2,1)}), bf16[1,2,16,1,20,1536]{5,1,4,3,0,2:T(2,128)(2,1)S(1)}, u32[]{:S(2)}, u32[]{:S(2)}) async-start(bf16[1,2,16,1,20,1536]{5,1,4,3,0,2:T(2,128)(2,1)} %copy.15), calls=%async_computation.1 | async-start | bytes 3932160 | tf_op jit(solution)/sharding_constraint;jit(solution)/sharding_constraint | solution.py:13
  157.9 0.0 copy-done.6
  157.9 0.1 copy.10
  158.1 0.0 copy-done.3
  158.1 0.0 copy-done.5
  158.1 3.9 %convolution_convert_fusion.2 = bf16[256,32,20]{1,2,0:T(8,128)(2,1)} fusion(s32[256,2]{1,0:T(8,128)S(1)} %copy-done.3, s32[256,2]{1,0:T(8,128)S(1)} %copy-done.5, bf16[256,2]{1,0:T(8,128)(2,1)S(1)} %copy.10), kind=kOutput, calls=%fused_computation.27 | convolution fusion | flops 862208 | bytes 332800 | tf_op jit(solution)/abtke,abtkc->abtec/dot_general | solution.py:8
  162.0 22.8 %all-to-all-done.1 = bf16[1,2,16,1,20,1536]{5,1,4,3,0,2:T(2,128)(2,1)S(1)} async-done(((bf16[1,2,16,1,20,1536]{5,1,4,3,0,2:T(2,128)(2,1)}), bf16[1,2,16,1,20,1536]{5,1,4,3,0,2:T(2,128)(2,1)S(1)}, u32[]{:S(2)}, u32[]{:S(2)}) %all-to-all-start.1) | async-done | bytes 1966112 | tf_op jit(solution)/sharding_constraint;jit(solution)/sharding_constraint | solution.py:13
  184.8 3.3 %copy.16 = bf16[1,16,2,1,20,1536]{5,2,1,4,3,0:T(2,128)(2,1)} copy(bf16[1,16,2,1,20,1536]{5,2,4,3,0,1:T(2,128)(2,1)S(1)} %bitcast.155) | data formatting | bytes 3932160 | tf_op jit(solution)/sharding_constraint;jit(solution)/sharding_constraint | solution.py:13
  188.0 4.3 %reshape.77 = bf16[32,20,1536]{2,0,1:T(8,128)(2,1)S(1)} reshape(bf16[1,16,2,1,20,1536]{5,2,1,4,3,0:T(2,128)(2,1)} %copy.16) | data formatting | bytes 3932160
  192.3 0.0 copy-start.1
  192.3 3.4 %fusion.34 = bf16[1,1,256,1536]{3,2,1,0:T(8,128)(2,1)} fusion(bf16[32,20,1536]{2,0,1:T(8,128)(2,1)S(1)} %reshape.77, bf16[256,32,20]{1,2,0:T(8,128)(2,1)} %convolution_convert_fusion.2), kind=kOutput, calls=%fused_computation.21 | convolution fusion | flops 503709696 | bytes 3080192 | tf_op jit(solution)/abtec,aebcd->abtd/dot_general | solution.py:8
  195.7 0.0 copy-done.1
  (1 shorter events, 0.0 us)
Async XLA Ops:
  0.0 5.2 %copy-start = (bf16[1,1,256,1536]{3,2,1,0:T(8,128)(2,1)S(1)}, bf16[1,1,256,1536]{3,2,1,0:T(8,128)(2,1)}, u32[]{:S(2)}) copy-start(bf16[1,1,256,1536]{3,2,1,0:T(8,128)(2,1)} %param.3) | copy-start | bytes 2359300
  0.9 0.9 copy-start.2
  1.8 0.7 copy-start.4
  155.3 2.6 %copy-start.6 = (f32[1,1,256,2]{2,3,1,0:T(2,128)S(1)}, f32[1,1,256,2]{2,3,1,0:T(2,128)}, u32[]{:S(2)}) copy-start(f32[1,1,256,2]{2,3,1,0:T(2,128)} %param.1) | copy-start | bytes 6148
  155.3 2.8 %copy-start.3 = (s32[256,2]{1,0:T(8,128)S(1)}, s32[256,2]{1,0:T(8,128)}, u32[]{:S(2)}) copy-start(s32[256,2]{1,0:T(8,128)} %copy-done.2) | copy-start | bytes 6148
  155.3 2.8 %copy-start.5 = (s32[256,2]{1,0:T(8,128)S(1)}, s32[256,2]{1,0:T(8,128)}, u32[]{:S(2)}) copy-start(s32[256,2]{1,0:T(8,128)} %copy-done.4) | copy-start | bytes 6148
  155.3 29.5 %all-to-all-start.1 = ((bf16[1,2,16,1,20,1536]{5,1,4,3,0,2:T(2,128)(2,1)}), bf16[1,2,16,1,20,1536]{5,1,4,3,0,2:T(2,128)(2,1)S(1)}, u32[]{:S(2)}, u32[]{:S(2)}) async-start(bf16[1,2,16,1,20,1536]{5,1,4,3,0,2:T(2,128)(2,1)} %copy.15), calls=%async_computation.1 | async-start | bytes 3932160 | tf_op jit(solution)/sharding_constraint;jit(solution)/sharding_constraint | solution.py:13
  192.3 3.4 %copy-start.1 = (bf16[1,1,256,1536]{3,2,1,0:T(8,128)(2,1)S(1)}, bf16[1,1,256,1536]{3,2,1,0:T(8,128)(2,1)}, u32[]{:S(2)}) copy-start(bf16[1,1,256,1536]{3,2,1,0:T(8,128)(2,1)} %param.3) | copy-start | bytes 2359300
where the time goes:
time: 196 us
  matrix products  121 us (62%)
  blocking collectives  31.1 us (16%)
  waiting for transfers between devices  22.8 us (12%)
  local copies, waits for them, and re-layouts  18.1 us (9%)
  starting transfers between devices  2.59 us (1%)
    dot_general x7, matrix products, einsum(): return jnp.einsum(form, a.astype(jnp.float32), b.astype(jnp.float32))  121 us
    another operation x1, blocking collectives, placed(): return lax.with_sharding_constraint(v, NamedSharding(mesh, P(*spec)))  31.1 us
    another operation x1, waiting for transfers between devices, placed(): return lax.with_sharding_constraint(v, NamedSharding(mesh, P(*spec)))  22.8 us
    another operation x4, local copies, waits for them, and re-layouts, placed(): return lax.with_sharding_constraint(v, NamedSharding(mesh, P(*spec)))  11.3 us
    unnamed x15, local copies, waits for them, and re-layouts  4.94 us
  transfers between devices with their start and end apart: 1, of which 1 were waited for; matrix products, arithmetic and copies ran while one was open for 2% of the time, Pallas kernels for 0%

commit v1 on v0

v1 whole, which is shorter than its diff:
```python
import functools

import jax
import jax.numpy as jnp
from jax import lax
from jax.experimental import pallas as pl
from jax.experimental.pallas import tpu as pltpu
from jax.sharding import PartitionSpec as P

MESH = pl.DeviceIdType.MESH
F32, BF16 = jnp.float32, jnp.bfloat16

T, D, FF = 256, 1536, 9216
SLOTS = 20
GROUPS, PER = 2, 8
HALF = PER * SLOTS
ROWS = GROUPS * HALF
FC = 1536
NG = FF // FC
RG = 3
SUB = 256
NC = 512
NP = D // NC
KH = FF // 2
RD = 3
BLOCK = 80


def kernel(
    x_hbm, ex_hbm, sl_hbm, ga_hbm, wg, wu, wd, y_hbm,
    xb, exb, slb, gab, gbuf, ubuf, dbuf, h, z, snd, rcv, osnd, ret, cm, yacc, yb,
    insem, gsem, usem, dsem, ysem, ssem, rsem, ossem, orsem,
):
    me = lax.axis_index("ep")
    bits = [(me // w) % 2 for w in (8, 4, 2, 1)]

    def flips(g, jj):
        a, b = jj // 4, (jj // 2) % 2
        return a, b, (a + b + g) % 2, jj % 2

    def partner(g, jj):
        to = me
        for flip, bit, w in zip(flips(g, jj), bits, (8, 4, 2, 1)):
            if flip:
                to = to + (1 - 2 * bit) * w
        return to

    def g_copies(gi):
        e, i, s = gi // NG, gi % NG, gi % RG
        cols = pl.ds(pl.multiple_of(i * FC, FC), FC)
        return (
            pltpu.make_async_copy(wg.at[e, :, cols], gbuf.at[s], gsem.at[s]),
            pltpu.make_async_copy(wu.at[e, :, cols], ubuf.at[s], usem.at[s]),
        )

    def d_copy(di):
        e, p, half, s = di // (2 * NP), (di // 2) % NP, di % 2, di % RD
        return pltpu.make_async_copy(
            wd.at[e, pl.ds(pl.multiple_of(half * KH, KH), KH), pl.ds(pl.multiple_of(p * NC, NC), NC)],
            dbuf.at[s],
            dsem.at[s],
        )

    def dispatch_copy(e, g, jj):
        return pltpu.make_async_remote_copy(
            src_ref=snd.at[e, g, jj],
            dst_ref=rcv.at[e, g, jj],
            send_sem=ssem.at[e, g, jj],
            recv_sem=rsem.at[e, g, jj],
            device_id={"ep": partner(g, jj)} if isinstance(g, int) else {"ep": me},
            device_id_type=MESH,
        )

    def return_copy(e, p, g, jj):
        return pltpu.make_async_remote_copy(
            src_ref=osnd.at[e, p, g * PER + jj],
            dst_ref=ret.at[e, p, g * PER + jj],
            send_sem=ossem.at[e, p, g * PER + jj],
            recv_sem=orsem.at[e, p, g * PER + jj],
            device_id={"ep": partner(g, jj)},
            device_id_type=MESH,
        )

    partners = [(g, jj) for g in range(GROUPS) for jj in range(PER) if (g, jj) != (0, 0)]

    inputs = [
        pltpu.make_async_copy(a, b, insem.at[n])
        for n, (a, b) in enumerate(((ex_hbm, exb), (sl_hbm, slb), (ga_hbm, gab), (x_hbm, xb)))
    ]
    for c in inputs:
        c.start()
    for gi in range(RG):
        for c in g_copies(gi):
            c.start()
    for di in range(RD):
        d_copy(di).start()

    barrier = pltpu.get_barrier_semaphore()
    for g, jj in partners:
        pl.semaphore_signal(barrier, inc=1, device_id={"ep": partner(g, jj)}, device_id_type=MESH)
    for c in inputs:
        c.wait()

    key = jnp.where(slb[...] < SLOTS, exb[...] * 32 + slb[...], -1)
    key0 = jnp.broadcast_to(key[0:1], (16, T))
    key1 = jnp.broadcast_to(key[1:2], (16, T))
    row = lax.broadcasted_iota(jnp.int32, (16, T), 0)
    tile_of_row = lax.broadcasted_iota(jnp.int32, (16, 128), 0) // 4

    pl.semaphore_wait(barrier, len(partners))

    def dispatch(e, _):
        for g in range(GROUPS):
            marks = []
            for offset in (row, 16 + row % 4):
                for jj in range(PER):
                    want = offset + (2 * partner(g, jj) + e) * 32
                    hit = (key0 == want) | (key1 == want)
                    marks.append(jnp.where(hit, 1.0, 0.0).astype(BF16))
            marks = jnp.concatenate(marks, axis=0)
            for p in range(NP):
                v = jnp.dot(marks, xb[:, p * NC : (p + 1) * NC], preferred_element_type=F32)
                for jj in range(PER):
                    to = rcv if (g, jj) == (0, 0) else snd
                    for c in range(4):
                        part = v[jj * 16 : jj * 16 + 16, c * 128 : c * 128 + 128]
                        to[e, g, jj, p * BLOCK + c * 16 : p * BLOCK + c * 16 + 16, :] = part.astype(BF16)
                    rest = v[128 + jj * 16 : 128 + jj * 16 + 16]
                    part = rest[:, 0:128]
                    for c in range(1, 4):
                        part = jnp.where(tile_of_row == c, rest[:, c * 128 : c * 128 + 128], part)
                    to[e, g, jj, p * BLOCK + 64 : p * BLOCK + 80, :] = part.astype(BF16)
            for jj in range(PER):
                if (g, jj) != (0, 0):
                    dispatch_copy(e, g, jj).start()
        return 0

    lax.fori_loop(0, 2, dispatch, 0)

    def over_rows(v):
        v = jnp.transpose(jnp.broadcast_to(v, (128, T)))
        return jnp.concatenate([v, v], axis=1)

    keyf = key.astype(F32)
    k0, k1 = over_rows(keyf[0:1]), over_rows(keyf[1:2])
    g0, g1 = over_rows(gab[0:1]), over_rows(gab[1:2])
    lane = lax.broadcasted_iota(jnp.int32, (T, T), 1)
    j = lane // 16
    a, b = (j // 4) % 2, (j // 2) % 2
    flip = (a, b, (a + b + j // 8) % 2, j % 2)
    owner = sum(((f + bit) % 2) * w for f, bit, w in zip(flip, bits, (8, 4, 2, 1)))
    for e in range(2):
        for n, offset in enumerate((lane % 16, 16 + lane % 4)):
            want = ((2 * owner + e) * 32 + offset).astype(F32)
            v = jnp.where(k0 == want, g0, 0.0) + jnp.where(k1 == want, g1, 0.0)
            cm[e, n] = v.astype(BF16)

    def assemble(e, g):
        base = g * HALF
        for jj in range(PER):
            if jj == 0:

                @pl.when(g == 1)
                def _():
                    dispatch_copy(e, g, 0).wait_recv()
            else:
                dispatch_copy(e, g, jj).wait_recv()
        for jj in range(PER):
            for p in range(NP):
                for c in range(4):
                    z[pl.ds(pl.multiple_of(base + jj * 16, 16), 16), (p * 4 + c) * 128 : (p * 4 + c + 1) * 128] = rcv[
                        e, g, jj, p * BLOCK + c * 16 : p * BLOCK + c * 16 + 16, :
                    ]
        for quad in range(PER // 4):
            at = pl.ds(pl.multiple_of(base + 128 + quad * 16, 16), 16)
            for p in range(NP):
                rest = [rcv[e, g, quad * 4 + s, p * BLOCK + 64 : p * BLOCK + 80, :].astype(F32) for s in range(4)]
                for c in range(4):
                    v = jnp.concatenate([r[c * 4 : c * 4 + 4] for r in rest], axis=0)
                    z[at, (p * 4 + c) * 128 : (p * 4 + c + 1) * 128] = v.astype(BF16)

    def up(first, rows, i, s):
        at = pl.ds(first, rows)
        for n in range(FC // SUB):
            cols = slice(n * SUB, (n + 1) * SUB)
            gate = jnp.dot(z[at, :], gbuf[s, :, cols], preferred_element_type=F32)
            lift = jnp.dot(z[at, :], ubuf[s, :, cols], preferred_element_type=F32)
            v = gate / (1.0 + jnp.exp(-gate)) * lift
            h[at, pl.ds(pl.multiple_of(i * FC + n * SUB, SUB), SUB)] = v.astype(BF16)

    def early(g, _):
        assemble(0, g)

        def chunk(i, _):
            @pl.when(g == 0)
            def _():
                for c in g_copies(i):
                    c.wait()

            up(pl.multiple_of(g * HALF, 16), HALF, i, i)

            @pl.when(g == 1)
            def _():
                for c in g_copies(i + RG):
                    c.start()

            return 0

        return lax.fori_loop(0, RG, chunk, 0)

    lax.fori_loop(0, GROUPS, early, 0)

    def expert(e, _):
        @pl.when(e == 1)
        def _():
            def group(g, _):
                assemble(1, g)
                return 0

            lax.fori_loop(0, GROUPS, group, 0)

        def chunk(i, _):
            gi = e * NG + i
            for c in g_copies(gi):
                c.wait()
            up(0, ROWS, i, gi % RG)

            @pl.when(gi + RG < 2 * NG)
            def _():
                for c in g_copies(gi + RG):
                    c.start()

            return 0

        lax.fori_loop(RG - RG * e, NG, chunk, 0)

        def down(p, _):
            d0 = (e * NP + p) * 2
            d_copy(d0).wait()
            v = jnp.dot(h[:, 0:KH], dbuf[d0 % RD], preferred_element_type=F32)
            d_copy(d0 + 1).wait()
            v = jnp.dot(h[:, KH:FF], dbuf[(d0 + 1) % RD], preferred_element_type=F32) + v
            for g in range(GROUPS):
                for jj in range(PER):
                    to = ret if (g, jj) == (0, 0) else osnd
                    for c in range(4):
                        part = v[g * HALF + jj * 16 : g * HALF + jj * 16 + 16, c * 128 : c * 128 + 128]
                        to[e, p, g * PER + jj, c * 16 : c * 16 + 16, :] = part.astype(BF16)
                    rest = v[g * HALF + 128 + jj * 4 : g * HALF + 128 + jj * 4 + 4]
                    part = jnp.concatenate([rest[:, c * 128 : c * 128 + 128] for c in range(4)], axis=0)
                    to[e, p, g * PER + jj, 64:80, :] = part.astype(BF16)
            for g, jj in partners:
                return_copy(e, p, g, jj).start()
            for n in range(2):

                @pl.when(d0 + n + RD < 4 * NP)
                def _():
                    d_copy(d0 + n + RD).start()

            return 0

        return lax.fori_loop(0, NP, down, 0)

    lax.fori_loop(0, 2, expert, 0)

    tile_of = (lax.broadcasted_iota(jnp.int32, (T, 128), 0) // 4) % 4

    def total(n, _):
        e, p = n // NP, n % NP
        for g, jj in partners:
            return_copy(e, p, g, jj).wait_recv()
        main = jnp.concatenate(
            [ret[e, p, :, c * 16 : c * 16 + 16, :].reshape(T, 128) for c in range(4)], axis=1
        )
        rest = ret[e, p, :, 64:80, :].reshape(T, 128).astype(F32)
        rest = jnp.concatenate([jnp.where(tile_of == c, rest, 0.0).astype(BF16) for c in range(4)], axis=1)
        v = jnp.dot(cm[e, 0], main, preferred_element_type=F32) + jnp.dot(
            cm[e, 1], rest, preferred_element_type=F32
        )

        @pl.when(e == 0)
        def _():
            yacc[p] = v

        @pl.when(e == 1)
        def _():
            yb[p] = (yacc[p] + v).astype(BF16)
            pltpu.make_async_copy(
                yb.at[p], y_hbm.at[:, pl.ds(pl.multiple_of(p * NC, NC), NC)], ysem.at[p]
            ).start()

        return 0

    lax.fori_loop(0, 2 * NP, total, 0)

    for e in range(2):
        for g, jj in partners:
            dispatch_copy(e, g, jj).wait_send()
            for p in range(NP):
                return_copy(e, p, g, jj).wait_send()
    for p in range(NP):
        pltpu.make_async_copy(yb.at[p], y_hbm.at[:, p * NC : (p + 1) * NC], ysem.at[p]).wait()


def solution(mesh):
    dma = pltpu.SemaphoreType.DMA
    hbm = pl.BlockSpec(memory_space=pl.ANY)
    call = pl.pallas_call(
        kernel,
        out_shape=jax.ShapeDtypeStruct((T, D), BF16),
        in_specs=[hbm] * 7,
        out_specs=hbm,
        scratch_shapes=[
            pltpu.VMEM((T, D), BF16),
            pltpu.VMEM((2, T), jnp.int32),
            pltpu.VMEM((2, T), jnp.int32),
            pltpu.VMEM((2, T), F32),
            pltpu.VMEM((RG, D, FC), BF16),
            pltpu.VMEM((RG, D, FC), BF16),
            pltpu.VMEM((RD, KH, NC), BF16),
            pltpu.VMEM((ROWS, FF), BF16),
            pltpu.VMEM((ROWS, D), BF16),
            pltpu.VMEM((2, GROUPS, PER, NP * BLOCK, 128), BF16),
            pltpu.VMEM((2, GROUPS, PER, NP * BLOCK, 128), BF16),
            pltpu.VMEM((2, NP, GROUPS * PER, BLOCK, 128), BF16),
            pltpu.VMEM((2, NP, GROUPS * PER, BLOCK, 128), BF16),
            pltpu.VMEM((2, 2, T, T), BF16),
            pltpu.VMEM((NP, T, NC), F32),
            pltpu.VMEM((NP, T, NC), BF16),
            dma((4,)),
            dma((RG,)),
            dma((RG,)),
            dma((RD,)),
            dma((NP,)),
            dma((2, GROUPS, PER)),
            dma((2, GROUPS, PER)),
            dma((2, NP, GROUPS * PER)),
            dma((2, NP, GROUPS * PER)),
        ],
        compiler_params=pltpu.CompilerParams(
            collective_id=0, has_side_effects=True, vmem_limit_bytes=67043328
        ),
        name="moe",
    )

    def body(x, expert, slot, gate, w_gate, w_up, w_down):
        flat = [v.reshape(T, 2).T for v in (expert, slot, gate)]
        y = call(x.reshape(T, D), *flat, w_gate, w_up, w_down)
        return y.reshape(x.shape)

    tokens, experts = P("dp", "ep"), P("ep")
    return jax.shard_map(
        body, mesh=mesh, in_specs=(tokens,) * 4 + (experts,) * 3, out_specs=tokens, check_vma=False
    )
```

time: 196 us -> 97.4 us (0.50)
  matrix products: 121 us -> 0 us
  Pallas kernels: 0 us -> 95.1 us
  blocking collectives: 31.1 us -> 0 us
  waiting for transfers between devices: 22.8 us -> 0 us
  local copies, waits for them, and re-layouts: 18.1 us -> 2.06 us
  starting transfers between devices: 2.59 us -> 0 us
    dot_general x7 -> x0, matrix products: 121 us -> none  [einsum(): return jnp.einsum(form, a.astype(jnp.float32), b.astype(jnp.float32))]
    pallas_call x0 -> x1, Pallas kernels: none -> 95.1 us  [body(): y = call(x.reshape(T, D), *flat, w_gate, w_up, w_down)]
    another operation x1 -> x0, blocking collectives: 31.1 us -> none  [placed(): return lax.with_sharding_constraint(v, NamedSharding(mesh, P(*spec)))]
    another operation x1 -> x0, waiting for transfers between devices: 22.8 us -> none  [placed(): return lax.with_sharding_constraint(v, NamedSharding(mesh, P(*spec)))]
    another operation x4 -> x0, local copies, waits for them, and re-layouts: 11.3 us -> none  [placed(): return lax.with_sharding_constraint(v, NamedSharding(mesh, P(*spec)))]
    unnamed x15 -> x1, local copies, waits for them, and re-layouts: 4.94 us -> 2.06 us
    another operation x1 -> x0, starting transfers between devices: 2.59 us -> none  [placed(): return lax.with_sharding_constraint(v, NamedSharding(mesh, P(*spec)))]
  transfers between devices with their start and end apart: 1 -> 0, of which waited for: 1 -> 0; matrix products, arithmetic and copies ran while one was open for 2% -> 0% of each run, Pallas kernels for 0% -> 0%
where the time goes in v1:
time: 97.4 us; the launch traced here: 97.2 us
  Pallas kernels  95.1 us (98%)
  local copies, waits for them, and re-layouts  2.06 us (2%)
    pallas_call x1, Pallas kernels, body(): y = call(x.reshape(T, D), *flat, w_gate, w_up, w_down)  95.1 us
    unnamed x1, local copies, waits for them, and re-layouts  2.06 us

profile of v1, /device:TPU:0, one launch (start us, length us, event | category | flops | bytes accessed | tf_op | source)
XLA Modules:
  0.0 97.2 jit_solution(15414314479810791895)
XLA Ops:
  0.0 95.1 %moe.1 = bf16[256,1536]{1,0:T(8,128)(2,1)} custom-call(bf16[256,1536]{1,0:T(8,128)(2,1)} %bitcast.12, s32[2,256]{1,0:T(2,128)} %bitcast.13, s32[2,256]{1,0:T(2,128)} %bitcast.14, f32[2,256]{1,0:T(2,128)} %bitcast.15, bf16[2,1536,9216]{2,1,0:T(8,128)(2,1)} %wg.1, bf16[2,1536,9216]{2,1,0:T(8,128)(2,1)} %wu.1, bf16[2,9216,1536]{2,1,0:T(8,128)(2,1)} %wd.1), custom_call_target="tpu_custom_call" | custom-call | tf_op jit(solution)/shard_map/moe/pallas_call | solution.py:348
  95.1 2.1 %copy.9 = bf16[1,1,256,1536]{3,2,1,0:T(8,128)(2,1)} copy(bf16[1,1,256,1536]{3,2,1,0:T(8,128)(2,1)} %bitcast.11) | data formatting | bytes 1572864

commit v2 on v1

v2 whole, which is shorter than its diff:
```python
import functools

import jax
import jax.numpy as jnp
from jax import lax
from jax.experimental import pallas as pl
from jax.experimental.pallas import tpu as pltpu
from jax.sharding import PartitionSpec as P

MESH = pl.DeviceIdType.MESH
F32, BF16 = jnp.float32, jnp.bfloat16

T, D, FF = 256, 1536, 9216
SLOTS = 20
GROUPS, PER = 2, 8
HALF = PER * SLOTS
ROWS = GROUPS * HALF
FC = 1536
NG = FF // FC
EARLY = 4
SUB = 256
NC = 512
NP = D // NC
KH = FF // 2
PAIRS = NG + NP
RING = 5
BLOCK = 80


def kernel(
    x_hbm, ex_hbm, sl_hbm, ga_hbm, wg, wu, wd, y_hbm,
    xb, exb, slb, gab, wbuf, h, z, snd, rcv, ret, cm, yacc,
    insem, wsem, ysem, ssem, rsem, ossem, orsem,
):
    me = lax.axis_index("ep")
    bits = [(me // w) % 2 for w in (8, 4, 2, 1)]

    def flips(g, jj):
        return tuple(int(jj // 2 == n) ^ g for n in (3, 2, 1)) + (jj % 2,)

    def partner(g, jj):
        to = me
        for flip, bit, w in zip(flips(g, jj), bits, (8, 4, 2, 1)):
            if flip:
                to = to + (1 - 2 * bit) * w
        return to

    def load(q, half):
        e, r, s = q // PAIRS, q % PAIRS, q % RING

        @pl.when(r < NG)
        def _():
            for b in range(FC // NC):
                cols = pl.ds(pl.multiple_of(r * FC + b * NC, NC), NC)
                pltpu.make_async_copy(
                    (wg, wu)[half].at[e, :, cols], wbuf.at[s, half, pl.ds(b * D, D)], wsem.at[s, half]
                ).start()

        @pl.when(r >= NG)
        def _():
            cols = pl.ds(pl.multiple_of((r - NG) * NC, NC), NC)
            pltpu.make_async_copy(
                wd.at[e, pl.ds(half * KH, KH), cols], wbuf.at[s, half], wsem.at[s, half]
            ).start()

    def load_after(q, half):
        @pl.when(q + RING < 2 * PAIRS)
        def _():
            load(q + RING, half)

    def loaded(q, half):
        s = q % RING
        pltpu.make_async_copy(
            wd.at[0, pl.ds(0, KH), pl.ds(0, NC)], wbuf.at[s, half], wsem.at[s, half]
        ).wait()

    def dispatch_copy(e, g, jj):
        return pltpu.make_async_remote_copy(
            src_ref=snd.at[e, g, jj],
            dst_ref=rcv.at[e, g, jj],
            send_sem=ssem.at[e, g],
            recv_sem=rsem.at[e, g],
            device_id={"ep": partner(g, jj)},
            device_id_type=MESH,
        )

    def dispatch_wait(e, g, sem):
        first = 1 if g == 0 else 0
        pltpu.make_async_copy(snd.at[e, g, first:PER], rcv.at[e, g, first:PER], sem.at[e, g]).wait()

    def return_copy(e, p, g, jj):
        return pltpu.make_async_remote_copy(
            src_ref=snd.at[e, g, jj, pl.ds(p * BLOCK, BLOCK)],
            dst_ref=ret.at[e, p, g * PER + jj],
            send_sem=ossem.at[e, p],
            recv_sem=orsem.at[e, p],
            device_id={"ep": partner(g, jj)},
            device_id_type=MESH,
        )

    def return_wait(e, p, sem):
        blocks = slice(1, GROUPS * PER)
        pltpu.make_async_copy(ret.at[e, p, blocks], ret.at[e, p, blocks], sem.at[e, p]).wait()

    partners = [(g, jj) for g in range(GROUPS) for jj in range(PER) if (g, jj) != (0, 0)]

    inputs = [
        pltpu.make_async_copy(a, b, insem.at[n])
        for n, (a, b) in enumerate(((ex_hbm, exb), (sl_hbm, slb), (ga_hbm, gab), (x_hbm, xb)))
    ]
    for c in inputs:
        c.start()

    barrier = pltpu.get_barrier_semaphore()
    for g, jj in partners:
        pl.semaphore_signal(barrier, inc=1, device_id={"ep": partner(g, jj)}, device_id_type=MESH)
    with jax.named_scope("in_wait"):
        for c in inputs:
            c.wait()
    for q in range(RING):
        for half in range(2):
            load(q, half)

    key = jnp.where(slb[...] < SLOTS, exb[...] * 32 + slb[...], -1)
    key0 = jnp.broadcast_to(key[0:1], (16, T))
    key1 = jnp.broadcast_to(key[1:2], (16, T))
    row = lax.broadcasted_iota(jnp.int32, (16, T), 0)
    tile_of_row = lax.broadcasted_iota(jnp.int32, (16, 128), 0) // 4

    with jax.named_scope("barrier"):
        pl.semaphore_wait(barrier, len(partners))

    def dispatch(e, _):
        for g in range(GROUPS):
            marks = []
            for offset in (row, 16 + row % 4):
                for jj in range(PER):
                    want = offset + (2 * partner(g, jj) + e) * 32
                    hit = (key0 == want) | (key1 == want)
                    marks.append(jnp.where(hit, 1.0, 0.0).astype(BF16))
            marks = jnp.concatenate(marks, axis=0)
            for p in range(NP):
                v = jnp.dot(marks, xb[:, p * NC : (p + 1) * NC], preferred_element_type=F32)
                for jj in range(PER):
                    to = rcv if (g, jj) == (0, 0) else snd
                    for c in range(4):
                        part = v[jj * 16 : jj * 16 + 16, c * 128 : c * 128 + 128]
                        to[e, g, jj, p * BLOCK + c * 16 : p * BLOCK + c * 16 + 16, :] = part.astype(BF16)
                    rest = v[128 + jj * 16 : 128 + jj * 16 + 16]
                    part = rest[:, 0:128]
                    for c in range(1, 4):
                        part = jnp.where(tile_of_row == c, rest[:, c * 128 : c * 128 + 128], part)
                    to[e, g, jj, p * BLOCK + 64 : p * BLOCK + 80, :] = part.astype(BF16)

            @pl.when(e == 0)
            def _():
                if g == 1:
                    dispatch_wait(0, 0, ssem)
                for jj in range(PER):
                    if (g, jj) != (0, 0):
                        dispatch_copy(0, g, jj).start()

        return 0

    with jax.named_scope("dispatch"):
        lax.fori_loop(0, 2, dispatch, 0)

    def over_rows(v):
        v = jnp.transpose(jnp.broadcast_to(v, (128, T)))
        return jnp.concatenate([v, v], axis=1)

    keyf = key.astype(F32)
    k0, k1 = over_rows(keyf[0:1]), over_rows(keyf[1:2])
    g0, g1 = over_rows(gab[0:1]), over_rows(gab[1:2])
    lane = lax.broadcasted_iota(jnp.int32, (T, T), 1)
    j = lane // 16
    flip = [(jnp.where((j // 2) % 4 == n, 1, 0) + j // 8) % 2 for n in (3, 2, 1)] + [j % 2]
    owner = sum(((f + bit) % 2) * w for f, bit, w in zip(flip, bits, (8, 4, 2, 1)))
    for e in range(2):
        for n, offset in enumerate((lane % 16, 16 + lane % 4)):
            want = ((2 * owner + e) * 32 + offset).astype(F32)
            v = jnp.where(k0 == want, g0, 0.0) + jnp.where(k1 == want, g1, 0.0)
            cm[e, n] = v.astype(BF16)

    def assemble(e, g):
        base = g * HALF
        with jax.named_scope("rows_wait"):
            for n in range(GROUPS):

                @pl.when(g == n)
                def _():
                    dispatch_wait(e, n, rsem)

        for jj in range(PER):
            for p in range(NP):
                for c in range(4):
                    z[pl.ds(pl.multiple_of(base + jj * 16, 16), 16), (p * 4 + c) * 128 : (p * 4 + c + 1) * 128] = rcv[
                        e, g, jj, p * BLOCK + c * 16 : p * BLOCK + c * 16 + 16, :
                    ]
        for quad in range(PER // 4):
            at = pl.ds(pl.multiple_of(base + 128 + quad * 16, 16), 16)
            for p in range(NP):
                rest = [rcv[e, g, quad * 4 + s, p * BLOCK + 64 : p * BLOCK + 80, :].astype(F32) for s in range(4)]
                for c in range(4):
                    v = jnp.concatenate([r[c * 4 : c * 4 + 4] for r in rest], axis=0)
                    z[at, (p * 4 + c) * 128 : (p * 4 + c + 1) * 128] = v.astype(BF16)

    def up(first, rows, i, s):
        at = pl.ds(first, rows)
        for n in range(FC // SUB):
            depth, cols = slice(n // 2 * D, n // 2 * D + D), slice(n % 2 * SUB, n % 2 * SUB + SUB)
            gate = jnp.dot(z[at, :], wbuf[s, 0, depth, cols], preferred_element_type=F32)
            lift = jnp.dot(z[at, :], wbuf[s, 1, depth, cols], preferred_element_type=F32)
            v = gate / (1.0 + jnp.exp(-gate)) * lift
            h[at, pl.ds(pl.multiple_of(i * FC + n * SUB, SUB), SUB)] = v.astype(BF16)

    def early(g, _):
        assemble(0, g)

        @pl.when(g == 1)
        def _():
            for to in partners:
                dispatch_copy(1, *to).start()

        def chunk(i, _):
            @pl.when(g == 0)
            def _():
                loaded(i, 0)
                loaded(i, 1)

            with jax.named_scope("up_half"):
                up(pl.multiple_of(g * HALF, 16), HALF, i, i)

            @pl.when(g == 1)
            def _():
                load(i + RING, 0)
                load(i + RING, 1)

            return 0

        return lax.fori_loop(0, EARLY, chunk, 0)

    lax.fori_loop(0, GROUPS, early, 0)

    def expert(e, _):
        @pl.when(e == 1)
        def _():
            def group(g, _):
                assemble(1, g)
                return 0

            lax.fori_loop(0, GROUPS, group, 0)

        def chunk(i, _):
            q = e * PAIRS + i
            with jax.named_scope("up_wait"):
                loaded(q, 0)
                loaded(q, 1)
            with jax.named_scope("up_all"):
                up(0, ROWS, i, q % RING)
            load_after(q, 0)
            load_after(q, 1)
            return 0

        lax.fori_loop(EARLY - EARLY * e, NG, chunk, 0)

        @pl.when(e == 0)
        def _():
            dispatch_wait(0, 1, ssem)

        @pl.when(e == 1)
        def _():
            for g in range(GROUPS):
                dispatch_wait(1, g, ssem)

        def back(e, p, g, v):
            for jj in range(PER):
                own = (g, jj) == (0, 0)
                to = ret.at[e, p, 0] if own else snd.at[e, g, jj, pl.ds(pl.multiple_of(p * BLOCK, BLOCK), BLOCK)]
                for c in range(4):
                    part = v[jj * 16 : jj * 16 + 16, c * 128 : c * 128 + 128]
                    to[c * 16 : c * 16 + 16, :] = part.astype(BF16)
                rest = v[128 + jj * 4 : 128 + jj * 4 + 4]
                part = jnp.concatenate([rest[:, c * 128 : c * 128 + 128] for c in range(4)], axis=0)
                to[64:80, :] = part.astype(BF16)
            for jj in range(PER):
                if (g, jj) != (0, 0):
                    return_copy(e, p, g, jj).start()

        @pl.when(e == 0)
        def _():
            def down(p, _):
                q = NG + p
                loaded(q, 0)
                with jax.named_scope("down0"):
                    v = jnp.dot(h[:, 0:KH], wbuf[q % RING, 0], preferred_element_type=F32)
                load_after(q, 0)
                loaded(q, 1)
                with jax.named_scope("down1"):
                    v = jnp.dot(h[:, KH:FF], wbuf[q % RING, 1], preferred_element_type=F32) + v
                for g in range(GROUPS):
                    back(0, p, g, v[g * HALF : (g + 1) * HALF])
                load_after(q, 1)
                return 0

            lax.fori_loop(0, NP, down, 0)

        @pl.when(e == 1)
        def _():
            def down(p, _):
                q = PAIRS + NG + p
                loaded(q, 0)
                for g in (1, 0):
                    rows = slice(g * HALF, (g + 1) * HALF)
                    with jax.named_scope("half0"):
                        v = jnp.dot(h[rows, 0:KH], wbuf[q % RING, 0], preferred_element_type=F32)
                    if g == 1:
                        loaded(q, 1)
                    with jax.named_scope("half1"):
                        v = jnp.dot(h[rows, KH:FF], wbuf[q % RING, 1], preferred_element_type=F32) + v
                    back(1, p, g, v)
                return 0

            lax.fori_loop(0, NP, down, 0)

        return 0

    lax.fori_loop(0, 2, expert, 0)

    tile_of = (lax.broadcasted_iota(jnp.int32, (T, 128), 0) // 4) % 4

    def total(n, _):
        e, p = n // NP, n % NP
        with jax.named_scope("total_wait"):
            return_wait(e, p, orsem)
        main = jnp.concatenate(
            [ret[e, p, :, c * 16 : c * 16 + 16, :].reshape(T, 128) for c in range(4)], axis=1
        )
        rest = ret[e, p, :, 64:80, :].reshape(T, 128).astype(F32)
        rest = jnp.concatenate([jnp.where(tile_of == c, rest, 0.0).astype(BF16) for c in range(4)], axis=1)
        v = jnp.dot(cm[e, 0], main, preferred_element_type=F32) + jnp.dot(
            cm[e, 1], rest, preferred_element_type=F32
        )

        @pl.when(e == 0)
        def _():
            yacc[p] = v

        @pl.when(e == 1)
        def _():
            cols = pl.ds(pl.multiple_of(p * NC, NC), NC)
            xb[:, cols] = (yacc[p] + v).astype(BF16)
            pltpu.make_async_copy(xb.at[:, cols], y_hbm.at[:, cols], ysem.at[p]).start()

        return 0

    lax.fori_loop(0, 2 * NP, total, 0)

    with jax.named_scope("drain"):
        for e in range(2):
            for p in range(NP):
                return_wait(e, p, ossem)
        for p in range(NP):
            cols = slice(p * NC, (p + 1) * NC)
            pltpu.make_async_copy(xb.at[:, cols], y_hbm.at[:, cols], ysem.at[p]).wait()


def solution(mesh):
    dma = pltpu.SemaphoreType.DMA
    hbm = pl.BlockSpec(memory_space=pl.ANY)
    call = pl.pallas_call(
        kernel,
        out_shape=jax.ShapeDtypeStruct((T, D), BF16),
        in_specs=[hbm] * 7,
        out_specs=hbm,
        scratch_shapes=[
            pltpu.VMEM((T, D), BF16),
            pltpu.VMEM((2, T), jnp.int32),
            pltpu.VMEM((2, T), jnp.int32),
            pltpu.VMEM((2, T), F32),
            pltpu.VMEM((RING, 2, KH, NC), BF16),
            pltpu.VMEM((ROWS, FF), BF16),
            pltpu.VMEM((ROWS, D), BF16),
            pltpu.VMEM((2, GROUPS, PER, NP * BLOCK, 128), BF16),
            pltpu.VMEM((2, GROUPS, PER, NP * BLOCK, 128), BF16),
            pltpu.VMEM((2, NP, GROUPS * PER, BLOCK, 128), BF16),
            pltpu.VMEM((2, 2, T, T), BF16),
            pltpu.VMEM((NP, T, NC), F32),
            dma((4,)),
            dma((RING, 2)),
            dma((NP,)),
            dma((2, GROUPS)),
            dma((2, GROUPS)),
            dma((2, NP)),
            dma((2, NP)),
        ],
        compiler_params=pltpu.CompilerParams(
            collective_id=0, has_side_effects=True, vmem_limit_bytes=67043328
        ),
        name="moe",
    )

    def body(x, expert, slot, gate, w_gate, w_up, w_down):
        flat = [v.reshape(T, 2).T for v in (expert, slot, gate)]
        y = call(x.reshape(T, D), *flat, w_gate, w_up, w_down)
        return y.reshape(x.shape)

    tokens, experts = P("dp", "ep"), P("ep")
    return jax.shard_map(
        body, mesh=mesh, in_specs=(tokens,) * 4 + (experts,) * 3, out_specs=tokens, check_vma=False
    )
```

time: 97.4 us -> 82.2 us (0.84)
  Pallas kernels: 95.1 us -> 80 us
    pallas_call x1, Pallas kernels: 95.1 us -> 80 us  [body(): y = call(x.reshape(T, D), *flat, w_gate, w_up, w_down)]
where the time goes in v2:
time: 82.2 us; the launch traced here: 82 us
  Pallas kernels  80 us (97%)
  local copies, waits for them, and re-layouts  2.06 us (3%)
    pallas_call x1, Pallas kernels, body(): y = call(x.reshape(T, D), *flat, w_gate, w_up, w_down)  80 us
    unnamed x1, local copies, waits for them, and re-layouts  2.06 us

profile of v2, /device:TPU:0, one launch (start us, length us, event | category | flops | bytes accessed | tf_op | source)
XLA Modules:
  0.0 82.0 jit_solution(2550549492925895004)
XLA Ops:
  0.0 80.0 %moe.1 = bf16[256,1536]{1,0:T(8,128)(2,1)} custom-call(bf16[256,1536]{1,0:T(8,128)(2,1)} %bitcast.12, s32[2,256]{1,0:T(2,128)} %bitcast.13, s32[2,256]{1,0:T(2,128)} %bitcast.14, f32[2,256]{1,0:T(2,128)} %bitcast.15, bf16[2,1536,9216]{2,1,0:T(8,128)(2,1)} %wg.1, bf16[2,1536,9216]{2,1,0:T(8,128)(2,1)} %wu.1, bf16[2,9216,1536]{2,1,0:T(8,128)(2,1)} %wd.1), custom_call_target="tpu_custom_call" | custom-call | tf_op jit(solution)/shard_map/moe/pallas_call | solution.py:405
  80.0 2.1 %copy.9 = bf16[1,1,256,1536]{3,2,1,0:T(8,128)(2,1)} copy(bf16[1,1,256,1536]{3,2,1,0:T(8,128)(2,1)} %bitcast.11) | data formatting | bytes 1572864
